TPU v7x, 32 devices: a whole 2x2x4 slice. The times are simulated.
32 devices in a mesh: member: 8 (over y, x, core), tensor: 4 (over z).
Axes of the slice: x: 2, y: 2, z: 4, core: 2. Of those that a mesh axis runs over, the one named last changes fastest.
Arguments:
- prompt_acts: bfloat16 [128, 5120], P(None, 'member'), may hold values from -6 to 6
- gate_weight: bfloat16 [5120, 13824], P('member', 'tensor'), may hold values from -0.078125 to 0.078125
- up_weight: bfloat16 [5120, 13824], P('member', 'tensor'), may hold values from -0.078125 to 0.078125
- down_weight: bfloat16 [13824, 5120], P('tensor', 'member'), may hold values from -0.0546875 to 0.0546875
- d_table: bfloat16 [128, 3, 4, 5120], P('member'), may hold values from -6 to 6
- f_table: bfloat16 [128, 3, 4, 13824], P('member', None, None, 'tensor'), may hold values from -6 to 6
- seeds: int32 [64], P('member'), may hold values from 0 to 15
- fitness: float32 [64], P('member'), may hold values from -6 to 6
Outputs:
- outputs: bfloat16 [64, 128, 5120], P('member', None, 'tensor')
- delta_gate: bfloat16 [5120, 13824], P('member', 'tensor')
- delta_up: bfloat16 [5120, 13824], P('member', 'tensor')
- delta_down: bfloat16 [13824, 5120], P('tensor', 'member')
Inputs may be any that keep to these rules, and one draw needn't show every extreme that they name: Member m uses row (m // 8) * 16 + seeds[m] of both tables, a row in its own group's block.
All inputs are finite; a program needn't handle non-finite values.
Results may differ from a plain program's by a relative error of at most 0.025.
Values may be sent and summed in bfloat16 or wider, within the bound.
No kernel may reach another device: no remote copies, remote signals or barrier semaphores. Data moves between devices by JAX's collectives and lax.ppermute only.
A program may use at most 192 MiB of HBM per device.

v0:
```python
import math
import jax
import jax.numpy as jnp
from jax import lax
from jax.sharding import PartitionSpec as P

D = 5120
FFW = 13824
perturb_gain = 0.5


def shards(prompt_acts, gate_weight, up_weight, down_weight, d_table, f_table, seeds, fitness):
    members = seeds.shape[0]
    prompt_len = prompt_acts.shape[0]
    rank_size = d_table.shape[2]
    d_sel = jnp.take(d_table, seeds, axis=0)
    selected_factors = jnp.take(f_table, seeds, axis=0)
    d_slices = lax.all_to_all(d_sel, "member", split_axis=3, concat_axis=0, tiled=True)
    f_all, fit_all = (
        lax.all_gather(selected_factors, "member", axis=0, tiled=True),
        lax.all_gather(fitness.astype(jnp.bfloat16), "member", axis=0, tiled=True).astype(
            fitness.dtype
        ),
    )
    population = fit_all.shape[0]
    gate_part = jnp.dot(prompt_acts, gate_weight, preferred_element_type=jnp.float32)
    up_part = jnp.dot(prompt_acts, up_weight, preferred_element_type=jnp.float32)
    prompt_full = lax.all_gather(prompt_acts, "member", axis=1, tiled=True)
    gate_sum, up_sum = (
        lax.psum(gate_part.astype(jnp.bfloat16), "member").astype(jnp.float32),
        lax.psum(up_part.astype(jnp.bfloat16), "member").astype(jnp.float32),
    )
    in_factors = d_sel[:, :2].reshape(members * 2 * rank_size, D)
    proj_sum = jnp.dot(prompt_full, in_factors.T, preferred_element_type=jnp.float32)
    base_gate = gate_sum.astype(jnp.bfloat16)
    base_up = up_sum.astype(jnp.bfloat16)
    proj_inputs = (
        (proj_sum / math.sqrt(D)).astype(jnp.bfloat16).reshape(prompt_len, members, 2, rank_size)
    )
    perturbed = jnp.einsum(
        "pmkr,mkrf->mkpf", proj_inputs, selected_factors[:, :2], preferred_element_type=jnp.float32
    )
    gate = base_gate.astype(jnp.float32)[None] + perturb_gain * perturbed[:, 0]
    up = base_up.astype(jnp.float32)[None] + perturb_gain * perturbed[:, 1]
    hidden_state = (jax.nn.silu(gate) * up).astype(jnp.bfloat16)
    projection_here = jnp.einsum(
        "cdv,czv->cdz", hidden_state, selected_factors[:, 2], preferred_element_type=jnp.float32
    )
    proj_down = (lax.psum(projection_here, "tensor") / math.sqrt(FFW)).astype(jnp.bfloat16)
    hidden_rows = hidden_state.reshape(members * prompt_len, hidden_state.shape[2])
    partial_value = jnp.dot(
        hidden_rows,
        lax.all_gather(down_weight, "member", axis=1, tiled=True),
        preferred_element_type=jnp.float32,
    )
    summed = lax.psum_scatter(
        partial_value.astype(jnp.bfloat16), "tensor", scatter_dimension=1, tiled=True
    ).astype(jnp.float32)
    local_column_range = summed.shape[1]
    col_start = lax.axis_index("tensor") * local_column_range
    out_factor = lax.dynamic_slice_in_dim(d_sel[:, 2], col_start, local_column_range, 2)
    down_noise_delta = perturb_gain * jnp.einsum(
        "mpr,mrd->mpd", proj_down, out_factor, preferred_element_type=jnp.float32
    )
    outputs = (summed.reshape(members, prompt_len, local_column_range) + down_noise_delta).astype(
        jnp.bfloat16
    )
    mean = jnp.sum(fit_all) / population
    spread = jnp.sum((fit_all - mean) ** 2) / population
    score = (fit_all - mean) / jnp.sqrt(spread + 1.0)
    weighted = (d_slices.astype(jnp.float32) * score[:, None, None, None]).astype(jnp.bfloat16)
    scale = 1.0 / math.sqrt(population * rank_size)
    width_cols = weighted.shape[3]
    hidden_cols = f_all.shape[3]
    w_gate = weighted[:, 0].reshape(population * rank_size, width_cols)
    w_up = weighted[:, 1].reshape(population * rank_size, width_cols)
    w_down = weighted[:, 2].reshape(population * rank_size, width_cols)
    f_gate = f_all[:, 0].reshape(population * rank_size, hidden_cols)
    f_up = f_all[:, 1].reshape(population * rank_size, hidden_cols)
    down_factor_columns = f_all[:, 2].reshape(population * rank_size, hidden_cols)
    delta_gate = (jnp.dot(w_gate.T, f_gate, preferred_element_type=jnp.float32) * scale).astype(
        jnp.bfloat16
    )
    delta_up = (jnp.dot(w_up.T, f_up, preferred_element_type=jnp.float32) * scale).astype(
        jnp.bfloat16
    )
    delta_down = (
        jnp.dot(down_factor_columns.T, w_down, preferred_element_type=jnp.float32) * scale
    ).astype(jnp.bfloat16)
    return (outputs, delta_gate, delta_up, delta_down)


def solution(mesh):
    in_specs = (
        P(None, "member"),
        P("member", "tensor"),
        P("member", "tensor"),
        P("tensor", "member"),
        P("member", None, None, None),
        P("member", None, None, "tensor"),
        P("member"),
        P("member"),
    )
    out_specs = (
        P("member", None, "tensor"),
        P("member", "tensor"),
        P("member", "tensor"),
        P("tensor", "member"),
    )
    return jax.shard_map(shards, mesh=mesh, in_specs=in_specs, out_specs=out_specs, check_vma=False)
```

profile of v0, /device:TPU:0, one launch (start us, length us, event | category | flops | bytes accessed | tf_op | source)
XLA Modules:
  0.0 510.3 jit_solution(4729490581838769242)
XLA Ops:
  7.2 0.0 copy-start
  7.2 0.0 all-reduce.4.cloned.1.call-start
  7.2 4.3 convolution_convert_fusion.1
  11.5 0.0 copy-start.4
  11.5 4.2 convolution_convert_fusion.2
  15.6 0.0 all-reduce.4.cloned.1.call-update
  15.7 0.0 all-gather.4.cloned.1.call-start
  15.7 0.7 all-gather.4.cloned.1.call-update
  16.4 0.0 all-gather.6.cloned.1.call-start
  16.5 0.7 all-gather.6.cloned.1.call-update
  17.2 0.0 all-gather.8.cloned.1.call-start
  17.2 0.0 copy-done.4
  17.2 2.4 gather_fusion.1
  19.7 1.2 broadcast_select_fusion.1
  20.9 0.0 all-gather.8.cloned.1.call-update
  20.9 0.0 reduce-scatter.2.cloned.1.call-start
  21.0 0.0 copy-done
  21.0 2.3 gather_fusion
  23.3 1.8 broadcast_select_fusion
  25.1 0.0 copy-start.2
  25.1 0.2 slice.52
  25.3 1.0 reshape.64
  26.3 52.1 %all-reduce.4.cloned.1.call-done = (bf16[128,3456]{1,0:T(8,128)(2,1)}, bf16[128,3456]{1,0:T(8,128)(2,1)}) async-done(((bf16[128,3456]{1,0:T(8,128)(2,1)}, bf16[128,3456]{1,0:T(8,128)(2,1)}), (bf16[128,3456]{1,0:T(8,128)(2,1)}, bf16[128,3456]{1,0:T(8,128)(2,1)})) %all-reduce.4.cloned.1.call-update) | async-done | bytes 1769488 | tf_op jit(solution)/shard_map/psum | solution.py:31
  78.5 1.3 convert_element_type.69
  79.8 0.0 copy-start.3
  79.8 3.1 convert_element_type.73
  82.9 21.3 %all-gather.4.cloned.1.call-done = bf16[128,5120]{1,0:T(8,128)(2,1)} async-done(((bf16[128,640]{1,0:T(8,128)(2,1)}), bf16[128,5120]{1,0:T(8,128)(2,1)}) %all-gather.4.cloned.1.call-update) | async-done | bytes 1310736 | tf_op jit(solution)/shard_map/all_gather | solution.py:28
  104.2 2.1 fusion.12
  106.2 18.7 %fusion.13 = f32[8,2,128,3456]{3,2,1,0:T(8,128)} fusion(bf16[128,8,2,4]{0,3,2,1:T(4,128)(2,1)S(1)} %bitcast.104, bf16[8,3,4,3456]{3,2,1,0:T(4,128)(2,1)} %broadcast_select_fusion.1), kind=kOutput, calls=%fused_computation.34 | convolution fusion | flops 56623104 | bytes 28770304 | tf_op jit(solution)/shard_map/pmkr,mkrf->mkpf/dot_general | solution.py:40
  125.0 11.1 %fusion = f32[8,1,128,3456]{3,2,0,1:T(8,128)} fusion(f32[8,2,128,3456]{3,2,1,0:T(8,128)} %fusion.13), kind=kLoop, calls=%fused_computation.4 | loop fusion | flops 3538944 | bytes 28311552 | tf_op jit(solution)/shard_map/mul | solution.py:43
  136.1 11.2 %slice_multiply_fusion = f32[8,1,128,3456]{3,2,1,0:T(8,128)} fusion(f32[8,2,128,3456]{3,2,1,0:T(8,128)} %fusion.13), kind=kLoop, calls=%fused_computation.2 | loop fusion | flops 3538944 | bytes 28311552 | tf_op jit(solution)/shard_map/mul | solution.py:44
  147.2 0.0 copy-done.3
  147.3 13.3 %fusion.4 = bf16[1024,3456]{1,0:T(8,128)(2,1)} fusion(f32[8,1,128,3456]{3,2,1,0:T(8,128)} %slice_multiply_fusion, f32[8,1,128,3456]{3,2,0,1:T(8,128)} %fusion, f32[128,3456]{1,0:T(8,128)} %convert_element_type.73, f32[128,3456]{1,0:T(8,128)S(1)} %convert_element_type.69), kind=kLoop, calls=%fused_computation.11 | loop fusion | flops 28311552 | bytes 38928384 | tf_op jit(solution)/shard_map/convert_element_type | solution.py:45
  160.6 114.7 %all-gather.6.cloned.1.call-done = bf16[3456,5120]{1,0:T(8,128)(2,1)} async-done(((bf16[3456,640]{1,0:T(8,128)(2,1)}), bf16[3456,5120]{1,0:T(8,128)(2,1)}) %all-gather.6.cloned.1.call-update) | async-done | bytes 35389456 | tf_op jit(solution)/shard_map/all_gather | solution.py:53
  275.2 45.1 %convolution_convert_fusion = bf16[1024,5120]{1,0:T(8,128)(2,1)} fusion(bf16[1024,3456]{1,0:T(8,128)(2,1)} %fusion.4, bf16[3456,5120]{1,0:T(8,128)(2,1)} %all-gather.6.cloned.1.call-done), kind=kOutput, calls=%fused_computation.13 | convolution fusion | flops 36244029440 | bytes 52953088 | tf_op jit(solution)/shard_map/dot_general | solution.py:51
  320.4 0.0 reduce-scatter.2.cloned.1.call-update
  320.4 14.9 %copy.34 = bf16[8,3,4,5120]{0,2,1,3:T(4,128)(2,1)} copy(bf16[8,3,4,5120]{3,2,1,0:T(4,128)(2,1)S(1)} %broadcast_select_fusion) | data formatting | bytes 1966080 | tf_op jit(solution)/shard_map/jit(_take)/select_n | solution.py:16
  335.3 0.0 copy-start.5
  335.3 0.0 copy-start.6
  335.3 19.3 %reshape.104 = bf16[8,2,30720]{2,1,0:T(2,128)(2,1)} reshape(bf16[5120,3,4,8]{3,2,1,0:T(4,128)(2,1)} %bitcast.102) | data formatting | bytes 1966080
  354.6 3.6 all-to-all-start
  358.2 0.0 copy-done.2
  358.2 0.0 copy-done.5
  358.2 0.0 copy-done.6
  358.2 0.7 dynamic-slice.1
  359.5 0.2 dynamic-update-slice
  359.8 19.9 %all-reduce = bf16[64]{0:T(256)(128)(2,1)S(1)} all-reduce(bf16[64]{0:T(256)(128)(2,1)S(1)} %dynamic-update-slice), channel_id=1, replica_groups=mesh['member'=8,'tensor'=4] {'member'}, use_global_device_ids=true, to_apply=%add | all-reduce | flops 64 | bytes 256
  379.7 0.7 convert_reduce_fusion
  381.0 0.7 multiply_reduce_fusion
  382.3 0.0 all-to-all-done
  382.3 19.7 %reshape.105 = bf16[5120,3,4,8]{3,2,1,0:T(4,128)(2,1)} reshape(bf16[8,2,30720]{2,1,0:T(2,128)(2,1)S(1)} %all-to-all-done) | data formatting | bytes 1966080
  402.1 19.0 %copy.35 = f32[8,3,4,8,640]{4,0,3,2,1:T(8,128)S(1)} copy(bf16[8,3,4,8,640]{0,2,1,4,3:T(4,128)(2,1)} %bitcast.101) | data formatting | bytes 2949120 | tf_op jit(solution)/shard_map/convert_element_type | solution.py:71
  421.1 0.2 fusion.11
  421.4 13.1 %fusion.8 = f32[8,128,4]{1,2,0:T(4,128)S(1)} fusion(f32[128,3456]{1,0:T(8,128)} %convert_element_type.73, f32[128,3456]{1,0:T(8,128)} %copy-done.3, bf16[8,3,4,3456]{3,2,1,0:T(4,128)(2,1)} %broadcast_select_fusion.1, f32[8,2,128,3456]{3,2,1,0:T(8,128)} %fusion.13), kind=kOutput, calls=%fused_computation.20 | convolution fusion | flops 63700992 | bytes 32088064 | tf_op jit(solution)/shard_map/cdv,czv->cdz/dot_general | solution.py:46
  434.4 20.0 %psum.23 = f32[8,128,4]{1,2,0:T(4,128)S(1)} all-reduce(f32[8,128,4]{1,2,0:T(4,128)S(1)} %fusion.8), channel_id=1, replica_groups=mesh['member'=8,'tensor'=4] {'tensor'}, use_global_device_ids=true, to_apply=%region_3.4 | all-reduce | flops 4096 | bytes 32768 | tf_op jit(solution)/shard_map/psum | solution.py:49
  454.4 0.0 all-gather.8.cloned.1.call-done
  454.4 3.6 fusion.23
  458.1 3.5 fusion.6
  461.5 3.5 fusion.7
  465.0 3.7 fusion.5
  468.7 30.9 %reduce-scatter.2.cloned.1.call-done = bf16[1024,1280]{1,0:T(8,128)(2,1)} async-done(((bf16[1024,5120]{1,0:T(8,128)(2,1)}), bf16[1024,1280]{1,0:T(8,128)(2,1)}) %reduce-scatter.2.cloned.1.call-update) | async-done | bytes 2621456 | tf_op jit(solution)/shard_map/reduce_scatter | solution.py:56
  499.6 0.0 slice-done
  499.6 4.2 fusion.10
  503.8 0.0 copy-done.1
  (8 shorter events, 0.0 us)
Async XLA Ops:
  7.2 13.8 %copy-start = (bf16[16,3,4,5120]{3,2,1,0:T(4,128)(2,1)S(1)}, bf16[16,3,4,5120]{3,2,1,0:T(4,128)(2,1)}, u32[]{:S(2)}) copy-start(bf16[16,3,4,5120]{3,2,1,0:T(4,128)(2,1)} %param.12) | copy-start | bytes 5898244
  7.2 71.3 %all-reduce.4.cloned.1.call-start = ((), (), s32[]{:S(2)}) async-start(), calls=%async_computation.6 | async-start | bytes 3538944 | tf_op jit(solution)/shard_map/psum | solution.py:31
  11.5 5.7 %copy-start.4 = (s32[8]{0:T(128)S(1)}, s32[8]{0:T(128)}, u32[]{:S(2)}) copy-start(s32[8]{0:T(128)} %param.14) | copy-start | bytes 100
  15.7 88.5 %all-gather.4.cloned.1.call-start = ((), (), s32[]{:S(2)}) async-start(), calls=%async_computation.2 | async-start | bytes 1474560 | tf_op jit(solution)/shard_map/all_gather | solution.py:28
  16.4 258.8 %all-gather.6.cloned.1.call-start = ((), (), s32[]{:S(2)}) async-start(), calls=%async_computation.3 | async-start | bytes 39813120 | tf_op jit(solution)/shard_map/all_gather | solution.py:53
  17.2 437.3 %all-gather.8.cloned.1.call-start = ((), (), s32[]{:S(2)}) async-start(), calls=%async_computation.5 | async-start | bytes 5971968 | tf_op jit(solution)/shard_map/all_gather | solution.py:20
  20.9 478.7 %reduce-scatter.2.cloned.1.call-start = ((), (), s32[]{:S(2)}) async-start(), calls=%async_computation.4 | async-start | bytes 13107200 | tf_op jit(solution)/shard_map/reduce_scatter | solution.py:56
  25.1 333.1 %copy-start.2 = (bf16[8,3,4,5120]{3,2,1,0:T(4,128)(2,1)}, bf16[8,3,4,5120]{3,2,1,0:T(4,128)(2,1)S(1)}, u32[]{:S(2)}) copy-start(bf16[8,3,4,5120]{3,2,1,0:T(4,128)(2,1)S(1)} %broadcast_select_fusion) | copy-start | bytes 2949124
  79.8 67.5 %copy-start.3 = (f32[128,3456]{1,0:T(8,128)}, f32[128,3456]{1,0:T(8,128)S(1)}, u32[]{:S(2)}) copy-start(f32[128,3456]{1,0:T(8,128)S(1)} %convert_element_type.69) | copy-start | bytes 5308420
  335.3 22.9 %copy-start.5 = (f32[8]{0:T(128)S(1)}, f32[8]{0:T(128)}, u32[]{:S(2)}) copy-start(f32[8]{0:T(128)} %param.15) | copy-start | bytes 100
  335.3 22.9 %copy-start.6 = (u32[32]{0:T(128)S(1)}, u32[32]{0:T(128)}, u32[]{:S(2)}) copy-start(u32[32]{0:T(128)} %constant.62) | copy-start | bytes 388
  354.6 27.7 %all-to-all-start = ((bf16[8,2,30720]{2,1,0:T(2,128)(2,1)}), bf16[8,2,30720]{2,1,0:T(2,128)(2,1)S(1)}, u32[]{:S(2)}, u32[]{:S(2)}) async-start(bf16[8,2,30720]{2,1,0:T(2,128)(2,1)} %reshape.104), calls=%async_computation.1 | async-start | bytes 1966080 | tf_op jit(solution)/shard_map/all_to_all | solution.py:18
  465.0 34.6 %slice-start = ((bf16[8,3,4,5120]{3,2,1,0:T(4,128)(2,1)}), bf16[8,1,4,5120]{3,2,1,0:T(4,128)(2,1)S(1)}, s32[]{:S(2)}) async-start(bf16[8,3,4,5120]{3,2,1,0:T(4,128)(2,1)} %copy-done.2), calls=%async_computation.7 | async-start | bytes 655360 | tf_op jit(solution)/shard_map/slice | solution.py:61
  465.0 38.8 %copy-start.1 = (bf16[16,3,4,5120]{3,2,1,0:T(4,128)(2,1)S(1)}, bf16[16,3,4,5120]{3,2,1,0:T(4,128)(2,1)}, u32[]{:S(2)}) copy-start(bf16[16,3,4,5120]{3,2,1,0:T(4,128)(2,1)} %param.12) | copy-start | bytes 5898244
Sparse Core Ops, SparseCore 0:
  15.8 62.6 all-reduce.3
  80.4 23.7 all-gather.3
  106.1 169.1 all-gather.5
  277.5 41.2 all-gather.7
  321.1 178.5 reduce-scatter.1
where the time goes:
time: 511 us; the launch traced here: 510 us
  waiting for transfers between devices  220 us (43%)
  matrix products  102 us (20%)
  local copies, waits for them, and re-layouts  83.5 us (16%)
  other arithmetic  44.6 us (9%)
  blocking collectives  39.9 us (8%)
  between operations  15.9 us (3%)
    all_gather x1, waiting for transfers between devices, shards(): lax.all_gather(down_weight, 'member', axis=1, tiled=True)  115 us
    psum x1, waiting for transfers between devices, shards(): lax.psum(up_part.astype(jnp.bfloat16), 'member').astype(jnp.float32)  52.1 us
    dot_general x1, matrix products, shards(): jnp.dot(hidden_rows, lax.all_gather(down_weight, 'member', axis=1, tiled=...  45.1 us
    unnamed x19, local copies, waits for them, and re-layouts  40 us
    reduce_scatter x1, waiting for transfers between devices, shards(): lax.psum_scatter(partial_value.astype(jnp.bfloat16), 'tensor', scatter_di...  30.9 us
    all_gather x1, waiting for transfers between devices, shards(): prompt_full = lax.all_gather(prompt_acts, 'member', axis=1, tiled=True)  21.3 us
    psum x1, blocking collectives, shards(): lax.psum(projection_here, 'tensor') / math.sqrt(FFW)  20 us
    unnamed x1, blocking collectives  19.9 us
  transfers between devices with their start and end apart: 6, of which 4 were waited for; matrix products, arithmetic and copies ran while one was open for 43% of the time, Pallas kernels for 0%

commit v1 on v0

--- a/solution.py
+++ b/solution.py
@@ -7,6 +7,13 @@
 D = 5120
 FFW = 13824
 perturb_gain = 0.5
+
+
+def swapped_in(block, axis, along):
+    size = lax.axis_size(axis)
+    shards = jnp.stack([block for _ in range(size)])
+    shards = lax.all_to_all(shards, axis, split_axis=0, concat_axis=0)
+    return jnp.concatenate(shards, axis=along)
 
 
 def shards(prompt_acts, gate_weight, up_weight, down_weight, d_table, f_table, seeds, fitness):
@@ -49,9 +56,7 @@
     proj_down = (lax.psum(projection_here, "tensor") / math.sqrt(FFW)).astype(jnp.bfloat16)
     hidden_rows = hidden_state.reshape(members * prompt_len, hidden_state.shape[2])
     partial_value = jnp.dot(
-        hidden_rows,
-        lax.all_gather(down_weight, "member", axis=1, tiled=True),
-        preferred_element_type=jnp.float32,
+        hidden_rows, swapped_in(down_weight, "member", 1), preferred_element_type=jnp.float32
     )
     summed = lax.psum_scatter(
         partial_value.astype(jnp.bfloat16), "tensor", scatter_dimension=1, tiled=True

time: 511 us -> 701 us (1.37)
  waiting for transfers between devices: 220 us -> 416 us
  other arithmetic: 44.6 us -> 21.3 us
  local copies, waits for them, and re-layouts: 83.5 us -> 104 us
  matrix products: 102 us -> 90.4 us
  starting transfers between devices: 3.75 us -> 11.1 us
    psum x1, waiting for transfers between devices: 52.1 us -> 310 us  [shards(): lax.psum(up_part.astype(jnp.bfloat16), 'member').astype(jnp.float32)]
    all_gather x1 -> x0, waiting for transfers between devices: 115 us -> none  [shards(): lax.all_gather(down_weight, 'member', axis=1, tiled=True)]
    all_to_all x0 -> x1, waiting for transfers between devices: none -> 39.1 us  [swapped_in(): shards = lax.all_to_all(shards, axis, split_axis=0, concat_axis=0)]
    mul x2 -> x0, other arithmetic: 22.2 us -> none  [the longest x1 11.2 us: shards(): up = base_up.astype(jnp.float32)[None] + perturb_gain * perturbed[:, 1]]
    another operation x0 -> x1, local copies, waits for them, and re-layouts: none -> 13.4 us  [swapped_in(): shards = jnp.stack([block for _ in range(size)])]
    dot_general x1, matrix products: 13.1 us -> 5.08 us  [shards(): jnp.einsum('cdv,czv->cdz', hidden_state, selected_factors[:, 2], preferre...]
    all_to_all x0 -> x1, starting transfers between devices: none -> 7.36 us  [swapped_in(): shards = lax.all_to_all(shards, axis, split_axis=0, concat_axis=0)]
    unnamed x19 -> x22, local copies, waits for them, and re-layouts: 40 us -> 47.2 us
  transfers between devices with their start and end apart: 6 -> 6, of which waited for: 4 -> 4; matrix products, arithmetic and copies ran while one was open for 43% -> 27% of each run, Pallas kernels for 0% -> 0%
where the time goes in v1:
time: 701 us; the launch traced here: 700 us
  waiting for transfers between devices  416 us (59%)
  local copies, waits for them, and re-layouts  104 us (15%)
  matrix products  90.4 us (13%)
  blocking collectives  40.8 us (6%)
  other arithmetic  21.3 us (3%)
  between operations  16 us (2%)
  starting transfers between devices  11.1 us (2%)
    psum x1, waiting for transfers between devices, shards(): lax.psum(up_part.astype(jnp.bfloat16), 'member').astype(jnp.float32)  310 us
    unnamed x22, local copies, waits for them, and re-layouts  47.2 us
    dot_general x1, matrix products, shards(): jnp.dot(hidden_rows, swapped_in(down_weight, 'member', 1), preferred_elem...  45.3 us
    all_to_all x1, waiting for transfers between devices, swapped_in(): shards = lax.all_to_all(shards, axis, split_axis=0, concat_axis=0)  39.1 us
    reduce_scatter x1, waiting for transfers between devices, shards(): lax.psum_scatter(partial_value.astype(jnp.bfloat16), 'tensor', scatter_di...  37.7 us
    all_gather x1, waiting for transfers between devices, shards(): prompt_full = lax.all_gather(prompt_acts, 'member', axis=1, tiled=True)  28.2 us
    psum x1, blocking collectives, shards(): lax.psum(projection_here, 'tensor') / math.sqrt(FFW)  20.9 us
    unnamed x1, blocking collectives  19.9 us
  transfers between devices with their start and end apart: 6, of which 4 were waited for; matrix products, arithmetic and copies ran while one was open for 27% of the time, Pallas kernels for 0%

profile of v1, /device:TPU:0, one launch (start us, length us, event | category | flops | bytes accessed | tf_op | source)
XLA Modules:
  0.0 699.8 jit_solution(15387109361979708764)
XLA Ops:
  7.2 0.0 copy-start
  7.2 7.3 %copy.43 = bf16[3456,640]{0,1:T(8,128)(2,1)} copy(bf16[3456,640]{1,0:T(8,128)(2,1)} %param.11) | data formatting | bytes 8847360 | tf_op args[3]
  14.5 13.4 %stack.2 = bf16[8,3456,640]{1,2,0:T(8,128)(2,1)} broadcast(bf16[3456,640]{0,1:T(8,128)(2,1)} %copy.43), dimensions={1,2} | broadcast | bytes 39813120 | tf_op jit(solution)/shard_map/stack | solution.py:14
  27.9 0.0 copy-start.4
  27.9 7.4 %all-to-all-start = ((bf16[8,3456,640]{1,2,0:T(8,128)(2,1)}), bf16[8,3456,640]{1,2,0:T(8,128)(2,1)}, u32[]{:S(2)}, u32[]{:S(2)}) async-start(bf16[8,3456,640]{1,2,0:T(8,128)(2,1)} %stack.2), calls=%async_computation | async-start | bytes 70778880 | tf_op jit(solution)/shard_map/all_to_all | solution.py:15
  35.3 0.0 all-reduce.4.cloned.1.call-start
  35.4 0.0 copy-done.4
  35.4 4.0 convolution_convert_fusion.1
  39.4 0.0 copy-start.5
  39.4 4.1 convolution_convert_fusion.2
  43.5 0.0 all-reduce.4.cloned.1.call-update
  43.5 0.0 all-gather.3.cloned.1.call-start
  43.6 0.7 all-gather.3.cloned.1.call-update
  44.3 0.0 all-gather.5.cloned.1.call-start
  44.3 0.0 copy-done.5
  44.3 2.4 gather_fusion.1
  46.8 1.2 broadcast_select_fusion.1
  48.0 0.0 all-gather.5.cloned.1.call-update
  48.0 0.0 reduce-scatter.2.cloned.1.call-start
  48.1 0.0 copy-done
  48.1 2.3 gather_fusion
  50.4 1.7 broadcast_select_fusion
  52.1 0.0 copy-start.2
  52.1 0.2 slice.52
  52.3 1.0 reshape.92
  53.3 310.3 %all-reduce.4.cloned.1.call-done = (bf16[128,3456]{1,0:T(8,128)(2,1)}, bf16[128,3456]{1,0:T(8,128)(2,1)}) async-done(((bf16[128,3456]{1,0:T(8,128)(2,1)}, bf16[128,3456]{1,0:T(8,128)(2,1)}), (bf16[128,3456]{1,0:T(8,128)(2,1)}, bf16[128,3456]{1,0:T(8,128)(2,1)})) %all-reduce.4.cloned.1.call-update) | async-done | bytes 1769488 | tf_op jit(solution)/shard_map/psum | solution.py:38
  363.6 1.3 convert_element_type.80
  364.9 2.5 convert_element_type.76
  367.3 28.2 %all-gather.3.cloned.1.call-done = bf16[128,5120]{1,0:T(8,128)(2,1)} async-done(((bf16[128,640]{1,0:T(8,128)(2,1)}), bf16[128,5120]{1,0:T(8,128)(2,1)}) %all-gather.3.cloned.1.call-update) | async-done | bytes 1310736 | tf_op jit(solution)/shard_map/all_gather | solution.py:35
  395.5 2.1 fusion.12
  397.6 0.0 copy-start.3
  397.6 15.0 %fusion.13 = f32[8,2,128,3456]{3,2,1,0:T(8,128)} fusion(bf16[128,8,2,4]{0,3,2,1:T(4,128)(2,1)S(1)} %bitcast.96, bf16[8,3,4,3456]{3,2,1,0:T(4,128)(2,1)} %broadcast_select_fusion.1), kind=kOutput, calls=%fused_computation.31 | convolution fusion | flops 56623104 | bytes 28770304 | tf_op jit(solution)/shard_map/pmkr,mkrf->mkpf/dot_general | solution.py:47
  412.6 0.0 copy-done.3
  412.6 13.2 %fusion.3 = bf16[8,128,3456]{2,1,0:T(8,128)(2,1)} fusion(f32[8,2,128,3456]{3,2,1,0:T(8,128)} %fusion.13, f32[128,3456]{1,0:T(8,128)S(1)} %convert_element_type.80, f32[128,3456]{1,0:T(8,128)S(1)} %copy-done.3), kind=kLoop, calls=%fused_computation.6 | loop fusion | flops 35389440 | bytes 38928384 | tf_op jit(solution)/shard_map/convert_element_type | solution.py:52
  425.9 39.1 %all-to-all-done = bf16[8,3456,640]{1,2,0:T(8,128)(2,1)} async-done(((bf16[8,3456,640]{1,2,0:T(8,128)(2,1)}), bf16[8,3456,640]{1,2,0:T(8,128)(2,1)}, u32[]{:S(2)}, u32[]{:S(2)}) %all-to-all-start) | async-done | bytes 35389472 | tf_op jit(solution)/shard_map/all_to_all | solution.py:15
  464.9 45.3 %convolution_convert_fusion = bf16[1024,5120]{1,0:T(8,128)(2,1)} fusion(bf16[1024,3456]{1,0:T(8,128)(2,1)} %bitcast.94, bf16[3456,5120]{0,1:T(8,128)(2,1)} %bitcast.7), kind=kOutput, calls=%fused_computation.11 | convolution fusion | flops 36244029440 | bytes 52953088 | tf_op jit(solution)/shard_map/dot_general | solution.py:58
  510.2 0.0 reduce-scatter.2.cloned.1.call-update
  510.2 14.9 %copy.44 = bf16[8,3,4,5120]{0,2,1,3:T(4,128)(2,1)} copy(bf16[8,3,4,5120]{3,2,1,0:T(4,128)(2,1)S(1)} %broadcast_select_fusion) | data formatting | bytes 1966080 | tf_op jit(solution)/shard_map/jit(_take)/select_n | solution.py:23
  525.2 0.0 copy-start.6
  525.2 0.0 copy-start.7
  525.2 19.3 %reshape.134 = bf16[8,2,30720]{2,1,0:T(2,128)(2,1)} reshape(bf16[5120,3,4,8]{3,2,1,0:T(4,128)(2,1)} %bitcast.93) | data formatting | bytes 1966080
  544.5 3.6 all-to-all-start.1
  548.0 0.0 copy-done.2
  548.1 0.0 copy-done.6
  548.1 0.0 copy-done.7
  548.1 0.6 dynamic-slice.1
  549.3 0.2 dynamic-update-slice
  549.6 19.9 %all-reduce = bf16[64]{0:T(256)(128)(2,1)S(1)} all-reduce(bf16[64]{0:T(256)(128)(2,1)S(1)} %dynamic-update-slice), channel_id=1, replica_groups=mesh['member'=8,'tensor'=4] {'member'}, use_global_device_ids=true, to_apply=%add | all-reduce | flops 64 | bytes 256
  569.5 0.6 convert_reduce_fusion
  570.8 0.6 multiply_reduce_fusion
  572.1 0.0 all-to-all-done.1
  572.1 19.7 %reshape.135 = bf16[5120,3,4,8]{3,2,1,0:T(4,128)(2,1)} reshape(bf16[8,2,30720]{2,1,0:T(2,128)(2,1)S(1)} %all-to-all-done.1) | data formatting | bytes 1966080
  591.8 19.0 %copy.45 = f32[8,3,4,8,640]{4,0,3,2,1:T(8,128)S(1)} copy(bf16[8,3,4,8,640]{0,2,1,4,3:T(4,128)(2,1)} %bitcast.92) | data formatting | bytes 2949120 | tf_op jit(solution)/shard_map/convert_element_type | solution.py:76
  610.9 0.2 fusion.11
  611.1 5.1 fusion.15
  616.2 20.9 %psum.23 = f32[8,128,4]{1,2,0:T(4,128)S(1)} all-reduce(f32[8,128,4]{1,2,0:T(4,128)S(1)} %fusion.15), channel_id=1, replica_groups=mesh['member'=8,'tensor'=4] {'tensor'}, use_global_device_ids=true, to_apply=%region_3.4 | all-reduce | flops 4096 | bytes 32768 | tf_op jit(solution)/shard_map/psum | solution.py:56
  637.1 3.7 fusion.22
  640.7 3.5 fusion.9
  644.2 3.5 fusion.8
  647.7 3.7 fusion.7
  651.4 37.7 %reduce-scatter.2.cloned.1.call-done = bf16[1024,1280]{1,0:T(8,128)(2,1)} async-done(((bf16[1024,5120]{1,0:T(8,128)(2,1)}), bf16[1024,1280]{1,0:T(8,128)(2,1)}) %reduce-scatter.2.cloned.1.call-update) | async-done | bytes 2621456 | tf_op jit(solution)/shard_map/reduce_scatter | solution.py:61
  689.1 0.0 slice-done
  689.1 4.2 fusion.10
  693.3 0.0 copy-done.1
  (9 shorter events, 0.0 us)
Async XLA Ops:
  7.2 40.9 %copy-start = (bf16[16,3,4,5120]{3,2,1,0:T(4,128)(2,1)S(1)}, bf16[16,3,4,5120]{3,2,1,0:T(4,128)(2,1)}, u32[]{:S(2)}) copy-start(bf16[16,3,4,5120]{3,2,1,0:T(4,128)(2,1)} %param.12) | copy-start | bytes 5898244
  27.9 7.4 %copy-start.4 = (bf16[128,640]{1,0:T(8,128)(2,1)S(1)}, bf16[128,640]{1,0:T(8,128)(2,1)}, u32[]{:S(2)}) copy-start(bf16[128,640]{1,0:T(8,128)(2,1)} %param.8) | copy-start | bytes 491524
  27.9 437.0 %all-to-all-start = ((bf16[8,3456,640]{1,2,0:T(8,128)(2,1)}), bf16[8,3456,640]{1,2,0:T(8,128)(2,1)}, u32[]{:S(2)}, u32[]{:S(2)}) async-start(bf16[8,3456,640]{1,2,0:T(8,128)(2,1)} %stack.2), calls=%async_computation | async-start | bytes 70778880 | tf_op jit(solution)/shard_map/all_to_all | solution.py:15
  35.3 328.3 %all-reduce.4.cloned.1.call-start = ((), (), s32[]{:S(2)}) async-start(), calls=%async_computation.6 | async-start | bytes 3538944 | tf_op jit(solution)/shard_map/psum | solution.py:38
  39.4 4.9 copy-start.5
  43.5 352.0 %all-gather.3.cloned.1.call-start = ((), (), s32[]{:S(2)}) async-start(), calls=%async_computation.3 | async-start | bytes 1474560 | tf_op jit(solution)/shard_map/all_gather | solution.py:35
  44.3 592.8 %all-gather.5.cloned.1.call-start = ((), (), s32[]{:S(2)}) async-start(), calls=%async_computation.5 | async-start | bytes 5971968 | tf_op jit(solution)/shard_map/all_gather | solution.py:27
  48.0 641.1 %reduce-scatter.2.cloned.1.call-start = ((), (), s32[]{:S(2)}) async-start(), calls=%async_computation.4 | async-start | bytes 13107200 | tf_op jit(solution)/shard_map/reduce_scatter | solution.py:61
  52.1 496.0 %copy-start.2 = (bf16[8,3,4,5120]{3,2,1,0:T(4,128)(2,1)}, bf16[8,3,4,5120]{3,2,1,0:T(4,128)(2,1)S(1)}, u32[]{:S(2)}) copy-start(bf16[8,3,4,5120]{3,2,1,0:T(4,128)(2,1)S(1)} %broadcast_select_fusion) | copy-start | bytes 2949124
  397.6 15.0 %copy-start.3 = (f32[128,3456]{1,0:T(8,128)S(1)}, f32[128,3456]{1,0:T(8,128)}, u32[]{:S(2)}) copy-start(f32[128,3456]{1,0:T(8,128)} %convert_element_type.76) | copy-start | bytes 5308420
  525.2 22.9 %copy-start.6 = (f32[8]{0:T(128)S(1)}, f32[8]{0:T(128)}, u32[]{:S(2)}) copy-start(f32[8]{0:T(128)} %param.15) | copy-start | bytes 100
  525.2 22.9 %copy-start.7 = (u32[32]{0:T(128)S(1)}, u32[32]{0:T(128)}, u32[]{:S(2)}) copy-start(u32[32]{0:T(128)} %constant.62) | copy-start | bytes 388
  544.5 27.6 %all-to-all-start.1 = ((bf16[8,2,30720]{2,1,0:T(2,128)(2,1)}), bf16[8,2,30720]{2,1,0:T(2,128)(2,1)S(1)}, u32[]{:S(2)}, u32[]{:S(2)}) async-start(bf16[8,2,30720]{2,1,0:T(2,128)(2,1)} %reshape.134), calls=%async_computation.2 | async-start | bytes 1966080 | tf_op jit(solution)/shard_map/all_to_all | solution.py:25
  647.7 41.4 %slice-start = ((bf16[8,3,4,5120]{3,2,1,0:T(4,128)(2,1)}), bf16[8,1,4,5120]{3,2,1,0:T(4,128)(2,1)S(1)}, s32[]{:S(2)}) async-start(bf16[8,3,4,5120]{3,2,1,0:T(4,128)(2,1)} %copy-done.2), calls=%async_computation.7 | async-start | bytes 655360 | tf_op jit(solution)/shard_map/slice | solution.py:66
  647.7 45.6 %copy-start.1 = (bf16[16,3,4,5120]{3,2,1,0:T(4,128)(2,1)S(1)}, bf16[16,3,4,5120]{3,2,1,0:T(4,128)(2,1)}, u32[]{:S(2)}) copy-start(bf16[16,3,4,5120]{3,2,1,0:T(4,128)(2,1)} %param.12) | copy-start | bytes 5898244
Sparse Core Ops, SparseCore 0:
  43.6 319.8 all-reduce.3
  365.5 29.9 all-gather.2
  398.0 62.7 all-gather.4
  510.4 178.7 reduce-scatter.1
